TPU v7x, 32 devices: a whole 2x2x4 slice. The times are simulated.
32 devices in a mesh: tok: 16 (over z, y, core), tp: 2 (over x).
Axes of the slice: x: 2, y: 2, z: 4, core: 2. Of those that a mesh axis runs over, the one named last changes fastest.
Arguments:
- hidden: bfloat16 [1536, 8192], P('tok'), may hold values from -2600 to 2600
- norm_gain: float32 [8192], replicated, may hold values from 0.5 to 1.5
- w_query: bfloat16 [8192, 4096], P('tok', 'tp'), may hold values from -1 to 1
- w_key: bfloat16 [8192, 1024], P('tok', 'tp'), may hold values from -1 to 1
- w_value: bfloat16 [8192, 1024], P('tok', 'tp'), may hold values from -0.0625 to 0.0625
- doc_ids: int32 [1536], P('tok'), may hold values from 0 to 3, as said below
Outputs:
- attended: bfloat16 [1536, 4096], P('tok', 'tp')
- out_scale: float32 [4096], P('tp')
- folded_gain: float32 [8192], P(('tok', 'tp'))
- codes_query: float32 [8192, 4096], P(('tok', 'tp'))
- codes_key: float32 [8192, 1024], P(('tok', 'tp'))
- codes_value: float32 [8192, 1024], P(('tok', 'tp'))
- scale_query: float32 [4096], P('tp')
- scale_key: float32 [1024], P('tp')
- scale_value: float32 [1024], P('tp')
Inputs may be any that keep to these rules, and one draw needn't show every extreme that they name: doc_ids never falls along the tokens; each of the 4 documents holds 1 to 1152 tokens and one holds exactly 1152.
All inputs are finite; a program needn't handle non-finite values. Where the computation divides by a largest or mean magnitude, that divisor is 1e-20 or more.
Results may differ from a plain program's by a relative error of at most 0.005.
The roundings to bfloat16 on the way count: a program that leaves them out, or rounds other values in their place, can miss the bound.
Values may be sent and summed in bfloat16 or wider, within the bound.
A program may use at most 128 MiB of HBM per device.

v0:
```python
import math
import jax
import jax.numpy as jnp
from jax import lax
from jax.sharding import PartitionSpec as P

HEAD = 128
KVH = 8
QHEADS = 32


def rotate(states, positions):
    half = states.shape[-1] // 2
    inverse = jnp.exp(
        jnp.arange(half, dtype=jnp.float32) * (-2.0 * math.log(10000.0) / states.shape[-1])
    )
    angles = positions[:, None] * inverse[None, :]
    cosine = jnp.cos(angles)[:, None, :]
    sine = jnp.sin(angles)[:, None, :]
    first = states[..., :half]
    second = states[..., half:]
    return jnp.concatenate(
        [first * cosine - second * sine, second * cosine + first * sine], axis=-1
    )


def smooth_from(input_peak, weight_peak):
    return jnp.sqrt(jnp.maximum(input_peak, 1e-05)) / jnp.sqrt(jnp.maximum(weight_peak, 1e-05))


def head_to_rows(matrix, tp_index, tp_count):
    sub_rows = matrix.shape[0] // tp_count
    columns = matrix.shape[1]
    whole = jnp.zeros((sub_rows, columns * tp_count), matrix.dtype)
    for shift in range(tp_count):
        target = lax.rem(tp_index + shift, tp_count)
        source = lax.rem(tp_index - shift + tp_count, tp_count)
        block = lax.dynamic_slice_in_dim(matrix, target * sub_rows, sub_rows)
        if shift > 0:
            pairs = [(i, (i + shift) % tp_count) for i in range(tp_count)]
            block = lax.ppermute(block, "tp", pairs)
        whole = lax.dynamic_update_slice_in_dim(whole, block, source * columns, axis=1)
    return whole


def on_device(hidden, norm_gain, w_query, w_key, w_value, doc_ids):
    tok_dev = hidden.shape[0]
    row_count = w_query.shape[0]
    tp_count = lax.axis_size("tp")
    tok_index = lax.axis_index("tok")
    tp_index = lax.axis_index("tp")
    heads_here = w_query.shape[1] // HEAD
    kv_here = w_key.shape[1] // HEAD
    group_size = QHEADS // KVH
    matrices = (w_query, w_key, w_value)
    states = hidden.astype(jnp.float32)
    normed = (
        states
        * lax.rsqrt(jnp.mean(states * states, axis=1, keepdims=True) + 1e-05)
        * norm_gain[None, :]
    ).astype(jnp.bfloat16)
    token_side = lax.all_to_all(normed, "tok", split_axis=1, concat_axis=0, tiled=True)
    input_rows = jnp.max(jnp.abs(token_side), axis=0).astype(jnp.float32)
    relaid = tuple((head_to_rows(matrix, tp_index, tp_count) for matrix in matrices))
    partial = jnp.dot(
        token_side, jnp.concatenate(matrices, axis=1), preferred_element_type=jnp.float32
    )
    summed = lax.psum_scatter(partial, "tok", scatter_dimension=0, tiled=True)
    query_columns, key_columns = (w_query.shape[1], w_key.shape[1])
    projected = (
        summed[:, :query_columns],
        summed[:, query_columns : query_columns + key_columns],
        summed[:, query_columns + key_columns :],
    )
    local_peak = jnp.max(
        jnp.stack([jnp.max(jnp.abs(matrix), axis=1) for matrix in matrices]), axis=0
    ).astype(jnp.float32)
    row_peak = lax.pmax(local_peak, "tp")
    smoothing_rows = smooth_from(input_rows, row_peak)
    column_local = tuple(
        (
            jnp.max(jnp.abs(smoothing_rows[:, None] * matrix.astype(jnp.float32)), axis=0)
            for matrix in matrices
        )
    )
    column_global = lax.pmax(column_local, "tok")
    scales = tuple((jnp.maximum(column, 1e-05) / 127.0 for column in column_global))
    query_positions = tok_index * tok_dev + jnp.arange(tok_dev, dtype=jnp.int32)
    positions = query_positions.astype(jnp.float32)
    query = (
        rotate(projected[0].reshape(tok_dev, heads_here, HEAD), positions)
        .astype(jnp.bfloat16)
        .reshape(tok_dev, kv_here, group_size, HEAD)
    )
    key = (
        rotate(projected[1].reshape(tok_dev, kv_here, HEAD), positions)
        .astype(jnp.bfloat16)
        .reshape(tok_dev, kv_here * HEAD)
    )
    value = projected[2].astype(jnp.bfloat16)
    score_scale = 1.0 / math.sqrt(HEAD)
    highest = jnp.full((kv_here, group_size, tok_dev), -1e30, jnp.float32)
    key_block = lax.all_gather(key, "tok", axis=0, tiled=True)
    value_block = lax.all_gather(value, "tok", axis=0, tiled=True)
    doc_block = lax.all_gather(doc_ids, "tok", axis=0, tiled=True)
    length = key_block.shape[0]
    scores = (
        jnp.einsum(
            "tkgd,skd->kgts",
            query,
            key_block.reshape(length, kv_here, HEAD),
            preferred_element_type=jnp.float32,
        )
        * score_scale
    )
    key_positions = jnp.arange(length, dtype=jnp.int32)
    allowed = (doc_ids[:, None] == doc_block[None, :]) & (
        key_positions[None, :] <= query_positions[:, None]
    )
    scores = jnp.where(allowed, scores, -1e30)
    raised = jnp.maximum(highest, jnp.max(scores, axis=3))
    weights = jnp.where(allowed, jnp.exp(scores - raised[..., None]), 0.0)
    totals = jnp.sum(weights, axis=3)
    accumulated = jnp.einsum(
        "kgts,skd->kgtd",
        weights.astype(jnp.bfloat16),
        value_block.reshape(length, kv_here, HEAD),
        preferred_element_type=jnp.float32,
    )
    highest, totals, accumulated = (raised, totals, accumulated)
    attended = (
        (accumulated / totals[..., None])
        .transpose(2, 0, 1, 3)
        .reshape(tok_dev, heads_here * HEAD)
        .astype(jnp.bfloat16)
    )
    out_scale = lax.pmax(jnp.max(jnp.abs(attended), axis=0).astype(jnp.float32), "tok")
    sub_rows = row_count // tp_count
    smooth_part = lax.dynamic_slice_in_dim(smoothing_rows, tp_index * sub_rows, sub_rows)
    gain_part = lax.dynamic_slice_in_dim(
        norm_gain, tok_index * row_count + tp_index * sub_rows, sub_rows
    )
    folded_gain = gain_part / smooth_part
    every_scale = lax.all_gather(scales, "tp", axis=0, tiled=True)
    codes = tuple(
        (
            smooth_part[:, None] * block.astype(jnp.float32) / column_scale[None, :]
            for block, column_scale in zip(relaid, every_scale)
        )
    )
    return (
        attended,
        out_scale,
        folded_gain,
        codes[0],
        codes[1],
        codes[2],
        scales[0],
        scales[1],
        scales[2],
    )


def solution(mesh):
    in_specs = (P("tok", None), P(), P("tok", "tp"), P("tok", "tp"), P("tok", "tp"), P("tok"))
    out_specs = (
        P("tok", "tp"),
        P("tp"),
        P(("tok", "tp")),
        P(("tok", "tp"), None),
        P(("tok", "tp"), None),
        P(("tok", "tp"), None),
        P("tp"),
        P("tp"),
        P("tp"),
    )
    return jax.shard_map(
        on_device, mesh=mesh, in_specs=in_specs, out_specs=out_specs, check_vma=False
    )
```

profile of v0, /device:TPU:0, one launch (start us, length us, event | category | flops | bytes accessed | tf_op | source)
XLA Modules:
  0.0 442.9 jit_solution(13857068211997247535)
XLA Ops:
  7.2 1.8 fusion.6
  9.1 1.9 fusion.8
  11.1 43.3 %all_to_all.19 = bf16[96,16,512]{2,0,1:T(8,128)(2,1)S(1)} all-to-all(bf16[96,16,512]{2,0,1:T(8,128)(2,1)S(1)} %bitcast.63), channel_id=1, replica_groups=mesh['tok'=16,'tp'=2] {'tok'}, dimensions={1} | all-to-all | bytes 3145728 | tf_op jit(solution)/shard_map/all_to_all | solution.py:62
  54.4 1.1 copy-done.2
  55.5 9.2 %fusion.9 = f32[1536,3072]{1,0:T(8,128)} fusion(bf16[1536,512]{1,0:T(8,128)(2,1)S(1)} %bitcast.62, bf16[512,512]{1,0:T(8,128)(2,1)S(1)} %copy-done.3, bf16[512,512]{1,0:T(8,128)(2,1)S(1)} %copy-done.4, bf16[512,2048]{1,0:T(8,128)(2,1)S(1)} %copy-done.1), kind=kOutput, calls=%fused_computation.14 | convolution fusion | flops 4841275392 | bytes 23592960 | tf_op jit(solution)/shard_map/dot_general | solution.py:65
  64.9 0.9 multiply_cosine_fusion
  65.8 193.7 %reduce-scatter.2.cloned.1.call-done = f32[96,3072]{1,0:T(8,128)} async-done(((f32[1536,3072]{1,0:T(8,128)}), f32[96,3072]{1,0:T(8,128)}) %reduce-scatter.2.cloned.1.call-update) | async-done | bytes 1179664 | tf_op jit(solution)/shard_map/reduce_scatter | solution.py:68
  259.4 0.9 slice.29
  260.4 1.0 subtract_convert_fusion.1
  261.6 0.7 copy.60
  262.4 0.9 broadcast.88.clone
  263.3 0.8 constant_dynamic-slice_fusion.1
  264.1 1.4 collective-permute-start.2
  265.5 0.8 broadcast.88.clone.1
  266.3 0.9 constant_dynamic-slice_fusion
  267.2 0.6 collective-permute-start.1
  267.8 1.6 broadcast_in_dim.18
  269.3 1.5 constant_dynamic-slice_fusion.2
  270.9 1.5 collective-permute-start
  272.4 0.6 dynamic-slice
  273.9 10.8 %all-reduce = s32[1536]{0:T(1024)} all-reduce(s32[1536]{0:T(1024)S(1)} %dynamic-update-slice), channel_id=1, replica_groups=mesh['tok'=16,'tp'=2] {'tok'}, use_global_device_ids=true, to_apply=%add | all-reduce | flops 1536 | bytes 12288
  284.8 0.7 abs_reduce_fusion.4
  285.5 1.0 abs_reduce_fusion.1
  286.5 0.9 fusion.32
  287.5 0.7 abs_reduce_fusion.5
  288.2 1.3 maximum_convert_fusion
  289.5 11.3 %pmax.36 = f32[512]{0:T(512)} all-reduce(f32[512]{0:T(512)} %maximum_convert_fusion), channel_id=1, replica_groups=mesh['tok'=16,'tp'=2] {'tp'}, use_global_device_ids=true, to_apply=%region_10.0 | all-reduce | flops 512 | bytes 4096 | tf_op jit(solution)/shard_map/pmax | solution.py:78
  300.8 1.7 constant_dynamic-update-slice_fusion
  302.5 1.7 constant_dynamic-update-slice_fusion.1
  304.2 2.3 constant_dynamic-update-slice_fusion.2
  306.5 1.6 slice.46
  308.1 1.7 fusion.16
  309.8 1.3 dynamic-slice_divide_fusion
  311.5 0.5 abs_reduce_fusion
  312.9 1.7 copy.32
  314.6 2.0 fusion
  316.6 3.6 copy-done
  320.2 2.8 fusion.1
  323.0 24.2 %all-gather.7.cloned.1.call-done = bf16[1536,512]{1,0:T(8,128)(2,1)} async-done(((bf16[96,512]{1,0:T(8,128)(2,1)}), bf16[1536,512]{1,0:T(8,128)(2,1)}) %all-gather.7.cloned.1.call-update) | async-done | bytes 1572880 | tf_op jit(solution)/shard_map/all_gather | solution.py:104
  347.2 2.4 reshape.131
  349.6 6.0 %abs_reduce_fusion.6 = (bf16[4,4,128]{2,1,0:T(4,128)(2,1)S(1)}, bf16[96,4,4,128]{3,0,2,1:T(8,128)(2,1)S(1)}) fusion(f32[96,4,4]{0,2,1:T(4,128)S(1)} %bitcast.72, bf16[1536,4,128,1]{2,1,0,3:T(4,128)(2,1)S(1)} %bitcast.65, f32[4,1536,96,4]{1,2,3,0:T(8,128)} %copy-done, f32[4,4,96]{2,1,0:T(4,128)S(1)} %broadcast_maximum_fusion, pred[96,1536]{1,0:T(8,128)(4,1)S(1)} %fusion.32), kind=kOutput, calls=%fused_computation.44 | convolution fusion | flops 616560640 | bytes 11567104 | tf_op jit(solution)/shard_map/kgts,skd->kgtd/dot_general | solution.py:124
  355.6 59.4 %all-reduce.1 = (f32[2048]{0:T(1024)}, f32[2048]{0:T(1024)S(1)}, f32[512]{0:T(512)S(1)}, f32[512]{0:T(512)S(1)}) all-reduce(bf16[2048]{0:T(1024)(128)(2,1)S(1)} %bitcast.75, f32[2048]{0:T(1024)S(1)} %abs_reduce_fusion, f32[512]{0:T(512)S(1)} %get-tuple-element.10, f32[512]{0:T(512)S(1)} %get-tuple-element.9), channel_id=1, replica_groups=mesh['tok'=16,'tp'=2] {'tok'}, use_global_device_ids=true, to_apply=%region_5.0 | all-reduce | flops 5120 | bytes 36864 | tf_op jit(solution)/shard_map/pmax | solution.py:137
  415.0 4.4 all-gather
  419.3 4.4 all-gather.1
  423.7 4.4 all_gather.21
  428.3 1.0 convert_element_type.67
  429.3 4.3 multiply_divide_fusion
  433.6 2.8 multiply_divide_fusion.1
  (57 shorter events, 2.2 us)
Async XLA Ops:
  7.2 252.2 %reduce-scatter.2.cloned.1.call-start = ((), (), s32[]{:S(2)}) async-start(), calls=%async_computation.2 | async-start | bytes 20054016 | tf_op jit(solution)/shard_map/reduce_scatter | solution.py:68
  10.9 44.6 %copy-start.1 = (bf16[512,2048]{1,0:T(8,128)(2,1)S(1)}, bf16[512,2048]{1,0:T(8,128)(2,1)}, u32[]{:S(2)}) copy-start(bf16[512,2048]{1,0:T(8,128)(2,1)} %param.8) | copy-start | bytes 6291460
  10.9 44.6 %copy-start.3 = (bf16[512,512]{1,0:T(8,128)(2,1)S(1)}, bf16[512,512]{1,0:T(8,128)(2,1)}, u32[]{:S(2)}) copy-start(bf16[512,512]{1,0:T(8,128)(2,1)} %param.10) | copy-start | bytes 1572868
  11.0 44.6 %copy-start.4 = (bf16[512,512]{1,0:T(8,128)(2,1)S(1)}, bf16[512,512]{1,0:T(8,128)(2,1)}, u32[]{:S(2)}) copy-start(bf16[512,512]{1,0:T(8,128)(2,1)} %param.9) | copy-start | bytes 1572868
  54.4 1.1 copy-start.2
  64.8 248.1 %all-gather.5.cloned.1.call-start = ((), (), s32[]{:S(2)}) async-start(), calls=%async_computation.3 | async-start | bytes 1671168 | tf_op jit(solution)/shard_map/all_gather | solution.py:103
  262.3 85.0 %all-gather.7.cloned.1.call-start = ((), (), s32[]{:S(2)}) async-start(), calls=%async_computation.4 | async-start | bytes 1671168 | tf_op jit(solution)/shard_map/all_gather | solution.py:104
  264.1 36.7 %collective-permute-start.2 = (bf16[256,512]{1,0:T(8,128)(2,1)S(1)}, bf16[256,512]{1,0:T(8,128)(2,1)}, u32[]{:S(2)}, u32[]{:S(2)}) collective-permute-start(bf16[256,512]{1,0:T(8,128)(2,1)S(1)} %get-tuple-element.21), channel_id=1, source_target_pairs={{0,1},{1,0},{2,3},{3,2},{4,5},{5,4},{6,7},{7,6},{8,9},{9,8},{10,11... | collective-permute-start | bytes 786440 | tf_op jit(solution)/shard_map/ppermute | solution.py:41
  267.2 35.3 %collective-permute-start.1 = (bf16[256,512]{1,0:T(8,128)(2,1)}, bf16[256,512]{1,0:T(8,128)(2,1)}, u32[]{:S(2)}, u32[]{:S(2)}) collective-permute-start(bf16[256,512]{1,0:T(8,128)(2,1)} %get-tuple-element.23), channel_id=1, source_target_pairs={{0,1},{1,0},{2,3},{3,2},{4,5},{5,4},{6,7},{7,6},{8,9},{9,8},{10,11... | collective-permute-start | bytes 786440 | tf_op jit(solution)/shard_map/ppermute | solution.py:41
  267.8 4.6 %copy-start.13 = (u32[32]{0:T(128)S(1)}, u32[32]{0:T(128)}, u32[]{:S(2)}) copy-start(u32[32]{0:T(128)} %constant.69) | copy-start | bytes 388
  267.8 5.9 %copy-start.12 = (s32[96]{0:T(128)S(1)}, s32[96]{0:T(128)}, u32[]{:S(2)}) copy-start(s32[96]{0:T(128)} %param.11) | copy-start | bytes 1156
  270.9 33.3 %collective-permute-start = (bf16[256,2048]{1,0:T(8,128)(2,1)}, bf16[256,2048]{1,0:T(8,128)(2,1)}, u32[]{:S(2)}, u32[]{:S(2)}) collective-permute-start(bf16[256,2048]{1,0:T(8,128)(2,1)} %get-tuple-element.17), channel_id=1, source_target_pairs={{0,1},{1,0},{2,3},{3,2},{4,5},{5,4},{6,7},{7,6},{8,9},{9,8},{10,11... | collective-permute-start | bytes 3145736 | tf_op jit(solution)/shard_map/ppermute | solution.py:41
  300.8 9.0 %copy-start.11 = (f32[512]{0:T(512)S(1)}, f32[512]{0:T(512)}, u32[]{:S(2)}) copy-start(f32[512]{0:T(512)} %pmax.36) | copy-start | bytes 6148
  308.1 3.9 copy-start.5
  311.2 1.1 copy-start.6
  311.2 1.1 copy-start.7
  316.6 3.6 copy-start
  415.0 18.6 %copy-start.9 = (f32[512]{0:T(512)}, f32[512]{0:T(512)S(1)}, u32[]{:S(2)}) copy-start(f32[512]{0:T(512)S(1)} %maximum_multiply_fusion.2) | copy-start | bytes 6148
  419.3 14.3 %copy-start.10 = (f32[512]{0:T(512)}, f32[512]{0:T(512)S(1)}, u32[]{:S(2)}) copy-start(f32[512]{0:T(512)S(1)} %maximum_multiply_fusion.1) | copy-start | bytes 6148
  423.7 9.9 %copy-start.8 = (f32[2048]{0:T(1024)}, f32[2048]{0:T(1024)S(1)}, u32[]{:S(2)}) copy-start(f32[2048]{0:T(1024)S(1)} %maximum_multiply_fusion) | copy-start | bytes 24580
Sparse Core Ops, SparseCore 0:
  64.9 194.4 reduce-scatter.1
  262.4 38.6 all-gather.4
  308.3 38.9 all-gather.6
where the time goes:
time: 444 us; the launch traced here: 443 us
  waiting for transfers between devices  218 us (49%)
  blocking collectives  138 us (31%)
  local copies, waits for them, and re-layouts  27 us (6%)
  other arithmetic  24.6 us (6%)
  matrix products  17.2 us (4%)
  between operations  14.7 us (3%)
    reduce_scatter x1, waiting for transfers between devices, on_device(): summed = lax.psum_scatter(partial, 'tok', scatter_dimension=0, tiled=True)  194 us
    pmax x1, blocking collectives, on_device(): lax.pmax(jnp.max(jnp.abs(attended), axis=0).astype(jnp.float32), 'tok')  59.4 us
    all_to_all x1, blocking collectives, on_device(): lax.all_to_all(normed, 'tok', split_axis=1, concat_axis=0, tiled=True)  43.3 us
    all_gather x1, waiting for transfers between devices, on_device(): value_block = lax.all_gather(value, 'tok', axis=0, tiled=True)  24.2 us
    all_gather x3, blocking collectives, on_device(): every_scale = lax.all_gather(scales, 'tp', axis=0, tiled=True)  13.1 us
    pmax x1, blocking collectives, on_device(): row_peak = lax.pmax(local_peak, 'tp')  11.3 us
    unnamed x1, blocking collectives  10.8 us
    dot_general x1, matrix products, on_device(): jnp.dot(token_side, jnp.concatenate(matrices, axis=1), preferred_element_...  9.24 us
  transfers between devices with their start and end apart: 6, of which 2 were waited for; matrix products, arithmetic and copies ran while one was open for 7% of the time, Pallas kernels for 0%

commit v1 on v0

--- a/solution.py
+++ b/solution.py
@@ -101,7 +101,12 @@
     score_scale = 1.0 / math.sqrt(HEAD)
     highest = jnp.full((kv_here, group_size, tok_dev), -1e30, jnp.float32)
     key_block = lax.all_gather(key, "tok", axis=0, tiled=True)
-    value_block = lax.all_gather(value, "tok", axis=0, tiled=True)
+    ring = [value]
+    for hop in range(15):
+        ring.append(lax.ppermute(ring[-1], "tok", [(dev, (dev + 1) % 16) for dev in range(16)]))
+    value_block = jnp.roll(
+        jnp.concatenate(ring[::-1], axis=0), (lax.axis_index("tok") + 1) * ring[0].shape[0], axis=0
+    )
     doc_block = lax.all_gather(doc_ids, "tok", axis=0, tiled=True)
     length = key_block.shape[0]
     scores = (

time: 444 us -> 482 us (1.086)
  waiting for transfers between devices: 218 us -> 270 us
  blocking collectives: 138 us -> 132 us
    ppermute x0 -> x15, waiting for transfers between devices: none -> 80.8 us  [on_device(): lax.ppermute(ring[-1], 'tok', [(dev, (dev + 1) % 16) for dev in range(16)])]
    all_gather x1 -> x0, waiting for transfers between devices: 24.2 us -> none  [on_device(): value_block = lax.all_gather(value, 'tok', axis=0, tiled=True)]
    reduce_scatter x1, waiting for transfers between devices: 194 us -> 170 us  [on_device(): summed = lax.psum_scatter(partial, 'tok', scatter_dimension=0, tiled=True)]
    all_gather x1, waiting for transfers between devices: 0.02 us -> 19.6 us  [on_device(): key_block = lax.all_gather(key, 'tok', axis=0, tiled=True)]
    pmax x1, blocking collectives: 11.3 us -> 4.93 us  [on_device(): row_peak = lax.pmax(local_peak, 'tp')]
  transfers between devices with their start and end apart: 6 -> 20, of which waited for: 2 -> 17; matrix products, arithmetic and copies ran while one was open for 7% -> 5% of each run, Pallas kernels for 0% -> 0%
where the time goes in v1:
time: 482 us
  waiting for transfers between devices  270 us (56%)
  blocking collectives  132 us (27%)
  local copies, waits for them, and re-layouts  25.1 us (5%)
  other arithmetic  20 us (4%)
  between operations  15.5 us (3%)
  matrix products  14.9 us (3%)
    reduce_scatter x1, waiting for transfers between devices, on_device(): summed = lax.psum_scatter(partial, 'tok', scatter_dimension=0, tiled=True)  170 us
    ppermute x15, waiting for transfers between devices, on_device(): lax.ppermute(ring[-1], 'tok', [(dev, (dev + 1) % 16) for dev in range(16)])  80.8 us
    pmax x1, blocking collectives, on_device(): lax.pmax(jnp.max(jnp.abs(attended), axis=0).astype(jnp.float32), 'tok')  59.4 us
    all_to_all x1, blocking collectives, on_device(): lax.all_to_all(normed, 'tok', split_axis=1, concat_axis=0, tiled=True)  43.3 us
    all_gather x1, waiting for transfers between devices, on_device(): key_block = lax.all_gather(key, 'tok', axis=0, tiled=True)  19.6 us
    all_gather x3, blocking collectives, on_device(): every_scale = lax.all_gather(scales, 'tp', axis=0, tiled=True)  13.1 us
    unnamed x1, blocking collectives  11.6 us
  transfers between devices with their start and end apart: 20, of which 17 were waited for; matrix products, arithmetic and copies ran while one was open for 5% of the time, Pallas kernels for 0%

profile of v1, /device:TPU:0, one launch (start us, length us, event | category | flops | bytes accessed | tf_op | source)
XLA Modules:
  0.0 481.5 jit_solution(5598340029187787315)
XLA Ops:
  7.2 1.8 fusion.6
  9.1 1.9 fusion.8
  11.1 43.3 %all_to_all.19 = bf16[96,16,512]{2,0,1:T(8,128)(2,1)S(1)} all-to-all(bf16[96,16,512]{2,0,1:T(8,128)(2,1)S(1)} %bitcast.68), channel_id=1, replica_groups=mesh['tok'=16,'tp'=2] {'tok'}, dimensions={1} | all-to-all | bytes 3145728 | tf_op jit(solution)/shard_map/all_to_all | solution.py:62
  54.4 1.1 copy-done.1
  55.5 9.2 %fusion.9 = f32[1536,3072]{1,0:T(8,128)} fusion(bf16[1536,512]{1,0:T(8,128)(2,1)S(1)} %bitcast.67, bf16[512,512]{1,0:T(8,128)(2,1)S(1)} %copy-done.3, bf16[512,512]{1,0:T(8,128)(2,1)S(1)} %copy-done.4, bf16[512,2048]{1,0:T(8,128)(2,1)S(1)} %copy-done), kind=kOutput, calls=%fused_computation.14 | convolution fusion | flops 4841275392 | bytes 23592960 | tf_op jit(solution)/shard_map/dot_general | solution.py:65
  64.8 0.9 broadcast.88.clone
  66.6 1.5 collective-permute-start.17
  70.3 1.5 broadcast_in_dim.18
  71.8 1.6 constant_dynamic-slice_fusion.2
  73.5 1.5 collective-permute-start.15
  76.5 11.6 %all-reduce = s32[1536]{0:T(1024)S(1)} all-reduce(s32[1536]{0:T(1024)S(1)} %dynamic-update-slice), channel_id=1, replica_groups=mesh['tok'=16,'tp'=2] {'tok'}, use_global_device_ids=true, to_apply=%add | all-reduce | flops 1536 | bytes 12288
  88.4 0.9 multiply_cosine_fusion
  89.7 169.7 %reduce-scatter.2.cloned.1.call-done = f32[96,3072]{1,0:T(8,128)} async-done(((f32[1536,3072]{1,0:T(8,128)}), f32[96,3072]{1,0:T(8,128)}) %reduce-scatter.2.cloned.1.call-update) | async-done | bytes 1179664 | tf_op jit(solution)/shard_map/reduce_scatter | solution.py:68
  259.4 0.9 slice.46
  260.6 6.5 %collective-permute-done = bf16[96,512]{1,0:T(8,128)(2,1)S(1)} collective-permute-done((bf16[96,512]{1,0:T(8,128)(2,1)S(1)}, bf16[96,512]{1,0:T(8,128)(2,1)S(1)}, u32[]{:S(2)}, u32[]{:S(2)}) %collective-permute-start) | collective-permute-done | bytes 98336 | tf_op jit(solution)/shard_map/ppermute | solution.py:106
  267.9 6.6 %collective-permute-done.1 = bf16[96,512]{1,0:T(8,128)(2,1)S(1)} collective-permute-done((bf16[96,512]{1,0:T(8,128)(2,1)S(1)}, bf16[96,512]{1,0:T(8,128)(2,1)S(1)}, u32[]{:S(2)}, u32[]{:S(2)}) %collective-permute-start.1) | collective-permute-done | bytes 98336 | tf_op jit(solution)/shard_map/ppermute | solution.py:106
  274.5 4.9 %pmax.36 = f32[512]{0:T(512)S(1)} all-reduce(f32[512]{0:T(512)S(1)} %maximum_convert_fusion), channel_id=1, replica_groups=mesh['tok'=16,'tp'=2] {'tp'}, use_global_device_ids=true, to_apply=%region_10.0 | all-reduce | flops 512 | bytes 4096 | tf_op jit(solution)/shard_map/pmax | solution.py:78
  279.5 1.8 collective-permute-done.2
  281.2 1.7 constant_dynamic-update-slice_fusion.32
  283.0 5.0 %collective-permute-done.3 = bf16[96,512]{1,0:T(8,128)(2,1)S(1)} collective-permute-done((bf16[96,512]{1,0:T(8,128)(2,1)S(1)}, bf16[96,512]{1,0:T(8,128)(2,1)S(1)}, u32[]{:S(2)}, u32[]{:S(2)}) %collective-permute-start.3) | collective-permute-done | bytes 98336 | tf_op jit(solution)/shard_map/ppermute | solution.py:106
  288.0 1.7 constant_dynamic-update-slice_fusion.33
  289.7 5.0 %collective-permute-done.4 = bf16[96,512]{1,0:T(8,128)(2,1)S(1)} collective-permute-done((bf16[96,512]{1,0:T(8,128)(2,1)S(1)}, bf16[96,512]{1,0:T(8,128)(2,1)S(1)}, u32[]{:S(2)}, u32[]{:S(2)}) %collective-permute-start.4) | collective-permute-done | bytes 98336 | tf_op jit(solution)/shard_map/ppermute | solution.py:106
  294.8 2.4 constant_dynamic-update-slice_fusion.34
  297.2 4.2 collective-permute-done.5
  301.6 6.5 %collective-permute-done.6 = bf16[96,512]{1,0:T(8,128)(2,1)S(1)} collective-permute-done((bf16[96,512]{1,0:T(8,128)(2,1)S(1)}, bf16[96,512]{1,0:T(8,128)(2,1)S(1)}, u32[]{:S(2)}, u32[]{:S(2)}) %collective-permute-start.6) | collective-permute-done | bytes 98336 | tf_op jit(solution)/shard_map/ppermute | solution.py:106
  308.8 6.1 %collective-permute-done.7 = bf16[96,512]{1,0:T(8,128)(2,1)S(1)} collective-permute-done((bf16[96,512]{1,0:T(8,128)(2,1)S(1)}, bf16[96,512]{1,0:T(8,128)(2,1)S(1)}, u32[]{:S(2)}, u32[]{:S(2)}) %collective-permute-start.7) | collective-permute-done | bytes 98336 | tf_op jit(solution)/shard_map/ppermute | solution.py:106
  315.5 6.2 %collective-permute-done.8 = bf16[96,512]{1,0:T(8,128)(2,1)S(1)} collective-permute-done((bf16[96,512]{1,0:T(8,128)(2,1)S(1)}, bf16[96,512]{1,0:T(8,128)(2,1)S(1)}, u32[]{:S(2)}, u32[]{:S(2)}) %collective-permute-start.8) | collective-permute-done | bytes 98336 | tf_op jit(solution)/shard_map/ppermute | solution.py:106
  322.6 5.9 %collective-permute-done.9 = bf16[96,512]{1,0:T(8,128)(2,1)S(1)} collective-permute-done((bf16[96,512]{1,0:T(8,128)(2,1)S(1)}, bf16[96,512]{1,0:T(8,128)(2,1)S(1)}, u32[]{:S(2)}, u32[]{:S(2)}) %collective-permute-start.9) | collective-permute-done | bytes 98336 | tf_op jit(solution)/shard_map/ppermute | solution.py:106
  328.4 1.4 dynamic-slice_divide_fusion
  329.9 5.3 %collective-permute-done.10 = bf16[96,512]{1,0:T(8,128)(2,1)S(1)} collective-permute-done((bf16[96,512]{1,0:T(8,128)(2,1)S(1)}, bf16[96,512]{1,0:T(8,128)(2,1)S(1)}, u32[]{:S(2)}, u32[]{:S(2)}) %collective-permute-start.10) | collective-permute-done | bytes 98336 | tf_op jit(solution)/shard_map/ppermute | solution.py:106
  335.2 1.0 subtract_convert_fusion.1
  336.2 5.7 %collective-permute-done.11 = bf16[96,512]{1,0:T(8,128)(2,1)S(1)} collective-permute-done((bf16[96,512]{1,0:T(8,128)(2,1)S(1)}, bf16[96,512]{1,0:T(8,128)(2,1)S(1)}, u32[]{:S(2)}, u32[]{:S(2)}) %collective-permute-start.11) | collective-permute-done | bytes 98336 | tf_op jit(solution)/shard_map/ppermute | solution.py:106
  342.7 5.9 %collective-permute-done.12 = bf16[96,512]{1,0:T(8,128)(2,1)S(1)} collective-permute-done((bf16[96,512]{1,0:T(8,128)(2,1)S(1)}, bf16[96,512]{1,0:T(8,128)(2,1)S(1)}, u32[]{:S(2)}, u32[]{:S(2)}) %collective-permute-start.12) | collective-permute-done | bytes 98336 | tf_op jit(solution)/shard_map/ppermute | solution.py:106
  348.6 1.2 slice_bitcast_fusion
  350.0 5.4 %collective-permute-done.13 = bf16[96,512]{1,0:T(8,128)(2,1)S(1)} collective-permute-done((bf16[96,512]{1,0:T(8,128)(2,1)S(1)}, bf16[96,512]{1,0:T(8,128)(2,1)S(1)}, u32[]{:S(2)}, u32[]{:S(2)}) %collective-permute-start.13) | collective-permute-done | bytes 98336 | tf_op jit(solution)/shard_map/ppermute | solution.py:106
  357.6 4.6 collective-permute-done.14
  364.0 19.6 %all-gather.4.cloned.1.call-done = bf16[1536,512]{1,0:T(8,128)(2,1)} async-done(((bf16[96,512]{1,0:T(8,128)(2,1)}), bf16[1536,512]{1,0:T(8,128)(2,1)}) %all-gather.4.cloned.1.call-update) | async-done | bytes 1572880 | tf_op jit(solution)/shard_map/all_gather | solution.py:103
  383.6 1.7 copy.33
  385.3 3.1 fusion
  388.5 2.8 fusion.1
  391.3 2.6 abs_reduce_fusion.6
  393.9 59.4 %all-reduce.1 = (f32[2048]{0:T(1024)}, f32[2048]{0:T(1024)S(1)}, f32[512]{0:T(512)S(1)}, f32[512]{0:T(512)S(1)}) all-reduce(bf16[2048]{0:T(1024)(128)(2,1)S(1)} %bitcast.80, f32[2048]{0:T(1024)S(1)} %abs_reduce_fusion, f32[512]{0:T(512)S(1)} %copy-done.30, f32[512]{0:T(512)S(1)} %get-tuple-element.9), channel_id=1, replica_groups=mesh['tok'=16,'tp'=2] {'tok'}, use_global_device_ids=true, to_apply=%region_5.0 | all-reduce | flops 5120 | bytes 36864 | tf_op jit(solution)/shard_map/pmax | solution.py:142
  453.3 4.4 all-gather
  457.6 4.4 all-gather.1
  462.0 4.4 all_gather.17
  466.6 1.0 convert_element_type.67
  467.6 4.3 multiply_divide_fusion
  471.9 2.8 multiply_divide_fusion.1
  (160 shorter events, 13.1 us)
Async XLA Ops:
  7.2 252.2 %reduce-scatter.2.cloned.1.call-start = ((), (), s32[]{:S(2)}) async-start(), calls=%async_computation.2 | async-start | bytes 20054016 | tf_op jit(solution)/shard_map/reduce_scatter | solution.py:68
  10.9 44.6 %copy-start = (bf16[512,2048]{1,0:T(8,128)(2,1)S(1)}, bf16[512,2048]{1,0:T(8,128)(2,1)}, u32[]{:S(2)}) copy-start(bf16[512,2048]{1,0:T(8,128)(2,1)} %param.8) | copy-start | bytes 6291460
  10.9 44.6 %copy-start.3 = (bf16[512,512]{1,0:T(8,128)(2,1)S(1)}, bf16[512,512]{1,0:T(8,128)(2,1)}, u32[]{:S(2)}) copy-start(bf16[512,512]{1,0:T(8,128)(2,1)} %param.10) | copy-start | bytes 1572868
  11.0 44.6 %copy-start.4 = (bf16[512,512]{1,0:T(8,128)(2,1)S(1)}, bf16[512,512]{1,0:T(8,128)(2,1)}, u32[]{:S(2)}) copy-start(bf16[512,512]{1,0:T(8,128)(2,1)} %param.9) | copy-start | bytes 1572868
  64.8 318.9 %all-gather.4.cloned.1.call-start = ((), (), s32[]{:S(2)}) async-start(), calls=%async_computation.3 | async-start | bytes 1671168 | tf_op jit(solution)/shard_map/all_gather | solution.py:103
  66.6 214.7 %collective-permute-start.17 = (bf16[256,512]{1,0:T(8,128)(2,1)}, bf16[256,512]{1,0:T(8,128)(2,1)}, u32[]{:S(2)}, u32[]{:S(2)}) collective-permute-start(bf16[256,512]{1,0:T(8,128)(2,1)} %get-tuple-element.21), channel_id=1, source_target_pairs={{0,1},{1,0},{2,3},{3,2},{4,5},{5,4},{6,7},{7,6},{8,9},{9,8},{10,11... | collective-permute-start | bytes 786440 | tf_op jit(solution)/shard_map/ppermute | solution.py:41
  69.7 218.3 %collective-permute-start.16 = (bf16[256,512]{1,0:T(8,128)(2,1)}, bf16[256,512]{1,0:T(8,128)(2,1)}, u32[]{:S(2)}, u32[]{:S(2)}) collective-permute-start(bf16[256,512]{1,0:T(8,128)(2,1)} %get-tuple-element.23), channel_id=1, source_target_pairs={{0,1},{1,0},{2,3},{3,2},{4,5},{5,4},{6,7},{7,6},{8,9},{9,8},{10,11... | collective-permute-start | bytes 786440 | tf_op jit(solution)/shard_map/ppermute | solution.py:41
  73.5 221.3 %collective-permute-start.15 = (bf16[256,2048]{1,0:T(8,128)(2,1)}, bf16[256,2048]{1,0:T(8,128)(2,1)}, u32[]{:S(2)}, u32[]{:S(2)}) collective-permute-start(bf16[256,2048]{1,0:T(8,128)(2,1)} %get-tuple-element.17), channel_id=1, source_target_pairs={{0,1},{1,0},{2,3},{3,2},{4,5},{5,4},{6,7},{7,6},{8,9},{9,8},{10,11... | collective-permute-start | bytes 3145736 | tf_op jit(solution)/shard_map/ppermute | solution.py:41
  260.3 6.8 %collective-permute-start = (bf16[96,512]{1,0:T(8,128)(2,1)S(1)}, bf16[96,512]{1,0:T(8,128)(2,1)S(1)}, u32[]{:S(2)}, u32[]{:S(2)}) collective-permute-start(bf16[96,512]{1,0:T(8,128)(2,1)S(1)} %slice.46), channel_id=1, source_target_pairs={{0,2},{2,4},{4,6},{6,8},{8,10},{10,12},{12,14},{14,16},{16,18},{18... | collective-permute-start | bytes 294920 | tf_op jit(solution)/shard_map/ppermute | solution.py:106
  267.7 6.7 %collective-permute-start.1 = (bf16[96,512]{1,0:T(8,128)(2,1)S(1)}, bf16[96,512]{1,0:T(8,128)(2,1)S(1)}, u32[]{:S(2)}, u32[]{:S(2)}) collective-permute-start(bf16[96,512]{1,0:T(8,128)(2,1)S(1)} %collective-permute-done), channel_id=1, source_target_pairs={{0,2},{2,4},{4,6},{6,8},{8,10},{10,12},{12,14},{14,16},{16,18},{18... | collective-permute-start | bytes 294920 | tf_op jit(solution)/shard_map/ppermute | solution.py:106
  274.5 20.2 %copy-start.9 = (bf16[96,512]{1,0:T(8,128)(2,1)}, bf16[96,512]{1,0:T(8,128)(2,1)S(1)}, u32[]{:S(2)}) copy-start(bf16[96,512]{1,0:T(8,128)(2,1)S(1)} %collective-permute-done.1) | copy-start | bytes 294916
  274.5 6.7 %collective-permute-start.2 = (bf16[96,512]{1,0:T(8,128)(2,1)S(1)}, bf16[96,512]{1,0:T(8,128)(2,1)S(1)}, u32[]{:S(2)}, u32[]{:S(2)}) collective-permute-start(bf16[96,512]{1,0:T(8,128)(2,1)S(1)} %collective-permute-done.1), channel_id=1, source_target_pairs={{0,2},{2,4},{4,6},{6,8},{8,10},{10,12},{12,14},{14,16},{16,18},{18... | collective-permute-start | bytes 294920 | tf_op jit(solution)/shard_map/ppermute | solution.py:106
  279.5 22.0 %copy-start.2 = (bf16[96,16,512]{2,0,1:T(8,128)(2,1)S(1)}, bf16[96,16,512]{2,0,1:T(8,128)(2,1)}, u32[]{:S(2)}) copy-start(bf16[96,16,512]{2,0,1:T(8,128)(2,1)} %copy-done.1) | copy-start | bytes 4718596
  281.2 13.5 %copy-start.11 = (bf16[96,512]{1,0:T(8,128)(2,1)}, bf16[96,512]{1,0:T(8,128)(2,1)S(1)}, u32[]{:S(2)}) copy-start(bf16[96,512]{1,0:T(8,128)(2,1)S(1)} %collective-permute-done.2) | copy-start | bytes 294916
  281.2 6.7 %collective-permute-start.3 = (bf16[96,512]{1,0:T(8,128)(2,1)S(1)}, bf16[96,512]{1,0:T(8,128)(2,1)S(1)}, u32[]{:S(2)}, u32[]{:S(2)}) collective-permute-start(bf16[96,512]{1,0:T(8,128)(2,1)S(1)} %collective-permute-done.2), channel_id=1, source_target_pairs={{0,2},{2,4},{4,6},{6,8},{8,10},{10,12},{12,14},{14,16},{16,18},{18... | collective-permute-start | bytes 294920 | tf_op jit(solution)/shard_map/ppermute | solution.py:106
  288.0 6.7 %collective-permute-start.4 = (bf16[96,512]{1,0:T(8,128)(2,1)S(1)}, bf16[96,512]{1,0:T(8,128)(2,1)S(1)}, u32[]{:S(2)}, u32[]{:S(2)}) collective-permute-start(bf16[96,512]{1,0:T(8,128)(2,1)S(1)} %collective-permute-done.3), channel_id=1, source_target_pairs={{0,2},{2,4},{4,6},{6,8},{8,10},{10,12},{12,14},{14,16},{16,18},{18... | collective-permute-start | bytes 294920 | tf_op jit(solution)/shard_map/ppermute | solution.py:106
  294.7 6.9 %copy-start.15 = (bf16[96,512]{1,0:T(8,128)(2,1)}, bf16[96,512]{1,0:T(8,128)(2,1)S(1)}, u32[]{:S(2)}) copy-start(bf16[96,512]{1,0:T(8,128)(2,1)S(1)} %collective-permute-done.4) | copy-start | bytes 294916
  294.7 6.7 %collective-permute-start.5 = (bf16[96,512]{1,0:T(8,128)(2,1)S(1)}, bf16[96,512]{1,0:T(8,128)(2,1)S(1)}, u32[]{:S(2)}, u32[]{:S(2)}) collective-permute-start(bf16[96,512]{1,0:T(8,128)(2,1)S(1)} %collective-permute-done.4), channel_id=1, source_target_pairs={{0,2},{2,4},{4,6},{6,8},{8,10},{10,12},{12,14},{14,16},{16,18},{18... | collective-permute-start | bytes 294920 | tf_op jit(solution)/shard_map/ppermute | solution.py:106
  294.7 35.0 %slice-start = ((f32[96,3072]{1,0:T(8,128)}), f32[96,512]{1,0:T(8,128)S(1)}, s32[]{:S(2)}) async-start(f32[96,3072]{1,0:T(8,128)} %reduce-scatter.2.cloned.1.call-done), calls=%async_computation.4 | async-start | bytes 393216 | tf_op jit(solution)/shard_map/slice | solution.py:72
  301.5 6.7 %collective-permute-start.6 = (bf16[96,512]{1,0:T(8,128)(2,1)S(1)}, bf16[96,512]{1,0:T(8,128)(2,1)S(1)}, u32[]{:S(2)}, u32[]{:S(2)}) collective-permute-start(bf16[96,512]{1,0:T(8,128)(2,1)S(1)} %collective-permute-done.5), channel_id=1, source_target_pairs={{0,2},{2,4},{4,6},{6,8},{8,10},{10,12},{12,14},{14,16},{16,18},{18... | collective-permute-start | bytes 294920 | tf_op jit(solution)/shard_map/ppermute | solution.py:106
  308.2 6.7 %collective-permute-start.7 = (bf16[96,512]{1,0:T(8,128)(2,1)S(1)}, bf16[96,512]{1,0:T(8,128)(2,1)S(1)}, u32[]{:S(2)}, u32[]{:S(2)}) collective-permute-start(bf16[96,512]{1,0:T(8,128)(2,1)S(1)} %collective-permute-done.6), channel_id=1, source_target_pairs={{0,2},{2,4},{4,6},{6,8},{8,10},{10,12},{12,14},{14,16},{16,18},{18... | collective-permute-start | bytes 294920 | tf_op jit(solution)/shard_map/ppermute | solution.py:106
  314.9 14.8 %copy-start.21 = (bf16[96,512]{1,0:T(8,128)(2,1)}, bf16[96,512]{1,0:T(8,128)(2,1)S(1)}, u32[]{:S(2)}) copy-start(bf16[96,512]{1,0:T(8,128)(2,1)S(1)} %collective-permute-done.7) | copy-start | bytes 294916
  314.9 6.7 %collective-permute-start.8 = (bf16[96,512]{1,0:T(8,128)(2,1)S(1)}, bf16[96,512]{1,0:T(8,128)(2,1)S(1)}, u32[]{:S(2)}, u32[]{:S(2)}) collective-permute-start(bf16[96,512]{1,0:T(8,128)(2,1)S(1)} %collective-permute-done.7), channel_id=1, source_target_pairs={{0,2},{2,4},{4,6},{6,8},{8,10},{10,12},{12,14},{14,16},{16,18},{18... | collective-permute-start | bytes 294920 | tf_op jit(solution)/shard_map/ppermute | solution.py:106
  315.5 40.0 %copy-start.6 = (f32[96,64]{1,0:T(8,128)S(1)}, f32[96,64]{1,0:T(8,128)}, u32[]{:S(2)}) copy-start(f32[96,64]{1,0:T(8,128)} %get-tuple-element.30) | copy-start | bytes 73732
  321.7 8.1 %copy-start.23 = (bf16[96,512]{1,0:T(8,128)(2,1)}, bf16[96,512]{1,0:T(8,128)(2,1)S(1)}, u32[]{:S(2)}) copy-start(bf16[96,512]{1,0:T(8,128)(2,1)S(1)} %collective-permute-done.8) | copy-start | bytes 294916
  321.7 6.7 %collective-permute-start.9 = (bf16[96,512]{1,0:T(8,128)(2,1)S(1)}, bf16[96,512]{1,0:T(8,128)(2,1)S(1)}, u32[]{:S(2)}, u32[]{:S(2)}) collective-permute-start(bf16[96,512]{1,0:T(8,128)(2,1)S(1)} %collective-permute-done.8), channel_id=1, source_target_pairs={{0,2},{2,4},{4,6},{6,8},{8,10},{10,12},{12,14},{14,16},{16,18},{18... | collective-permute-start | bytes 294920 | tf_op jit(solution)/shard_map/ppermute | solution.py:106
  328.4 27.1 %copy-start.25 = (bf16[96,512]{1,0:T(8,128)(2,1)}, bf16[96,512]{1,0:T(8,128)(2,1)S(1)}, u32[]{:S(2)}) copy-start(bf16[96,512]{1,0:T(8,128)(2,1)S(1)} %collective-permute-done.9) | copy-start | bytes 294916
  328.4 6.7 %collective-permute-start.10 = (bf16[96,512]{1,0:T(8,128)(2,1)S(1)}, bf16[96,512]{1,0:T(8,128)(2,1)S(1)}, u32[]{:S(2)}, u32[]{:S(2)}) collective-permute-start(bf16[96,512]{1,0:T(8,128)(2,1)S(1)} %collective-permute-done.9), channel_id=1, source_target_pairs={{0,2},{2,4},{4,6},{6,8},{8,10},{10,12},{12,14},{14,16},{16,18},{18... | collective-permute-start | bytes 294920 | tf_op jit(solution)/shard_map/ppermute | solution.py:106
  335.2 20.3 %copy-start.27 = (bf16[96,512]{1,0:T(8,128)(2,1)}, bf16[96,512]{1,0:T(8,128)(2,1)S(1)}, u32[]{:S(2)}) copy-start(bf16[96,512]{1,0:T(8,128)(2,1)S(1)} %collective-permute-done.10) | copy-start | bytes 294916
  335.2 6.7 %collective-permute-start.11 = (bf16[96,512]{1,0:T(8,128)(2,1)S(1)}, bf16[96,512]{1,0:T(8,128)(2,1)S(1)}, u32[]{:S(2)}, u32[]{:S(2)}) collective-permute-start(bf16[96,512]{1,0:T(8,128)(2,1)S(1)} %collective-permute-done.10), channel_id=1, source_target_pairs={{0,2},{2,4},{4,6},{6,8},{8,10},{10,12},{12,14},{14,16},{16,18},{18... | collective-permute-start | bytes 294920 | tf_op jit(solution)/shard_map/ppermute | solution.py:106
  341.9 6.7 %collective-permute-start.12 = (bf16[96,512]{1,0:T(8,128)(2,1)S(1)}, bf16[96,512]{1,0:T(8,128)(2,1)S(1)}, u32[]{:S(2)}, u32[]{:S(2)}) collective-permute-start(bf16[96,512]{1,0:T(8,128)(2,1)S(1)} %collective-permute-done.11), channel_id=1, source_target_pairs={{0,2},{2,4},{4,6},{6,8},{8,10},{10,12},{12,14},{14,16},{16,18},{18... | collective-permute-start | bytes 294920 | tf_op jit(solution)/shard_map/ppermute | solution.py:106
  348.6 6.8 %collective-permute-start.13 = (bf16[96,512]{1,0:T(8,128)(2,1)S(1)}, bf16[96,512]{1,0:T(8,128)(2,1)S(1)}, u32[]{:S(2)}, u32[]{:S(2)}) collective-permute-start(bf16[96,512]{1,0:T(8,128)(2,1)S(1)} %collective-permute-done.12), channel_id=1, source_target_pairs={{0,2},{2,4},{4,6},{6,8},{8,10},{10,12},{12,14},{14,16},{16,18},{18... | collective-permute-start | bytes 294920 | tf_op jit(solution)/shard_map/ppermute | solution.py:106
  349.8 12.5 %copy-start.24 = (bf16[96,512]{1,0:T(8,128)(2,1)S(1)}, bf16[96,512]{1,0:T(8,128)(2,1)}, u32[]{:S(2)}) copy-start(bf16[96,512]{1,0:T(8,128)(2,1)} %copy-done.23) | copy-start | bytes 294916
  349.8 12.5 %copy-start.22 = (bf16[96,512]{1,0:T(8,128)(2,1)S(1)}, bf16[96,512]{1,0:T(8,128)(2,1)}, u32[]{:S(2)}) copy-start(bf16[96,512]{1,0:T(8,128)(2,1)} %copy-done.21) | copy-start | bytes 294916
  350.0 12.4 %copy-start.20 = (bf16[96,512]{1,0:T(8,128)(2,1)S(1)}, bf16[96,512]{1,0:T(8,128)(2,1)}, u32[]{:S(2)}) copy-start(bf16[96,512]{1,0:T(8,128)(2,1)} %copy-done.19) | copy-start | bytes 294916
  350.0 12.4 %copy-start.18 = (bf16[96,512]{1,0:T(8,128)(2,1)S(1)}, bf16[96,512]{1,0:T(8,128)(2,1)}, u32[]{:S(2)}) copy-start(bf16[96,512]{1,0:T(8,128)(2,1)} %copy-done.17) | copy-start | bytes 294916
  350.0 12.4 %copy-start.16 = (bf16[96,512]{1,0:T(8,128)(2,1)S(1)}, bf16[96,512]{1,0:T(8,128)(2,1)}, u32[]{:S(2)}) copy-start(bf16[96,512]{1,0:T(8,128)(2,1)} %copy-done.15) | copy-start | bytes 294916
  350.0 12.4 %copy-start.14 = (bf16[96,512]{1,0:T(8,128)(2,1)S(1)}, bf16[96,512]{1,0:T(8,128)(2,1)}, u32[]{:S(2)}) copy-start(bf16[96,512]{1,0:T(8,128)(2,1)} %copy-done.13) | copy-start | bytes 294916
  355.5 6.7 %collective-permute-start.14 = (bf16[96,512]{1,0:T(8,128)(2,1)S(1)}, bf16[96,512]{1,0:T(8,128)(2,1)S(1)}, u32[]{:S(2)}, u32[]{:S(2)}) collective-permute-start(bf16[96,512]{1,0:T(8,128)(2,1)S(1)} %collective-permute-done.13), channel_id=1, source_target_pairs={{0,2},{2,4},{4,6},{6,8},{8,10},{10,12},{12,14},{14,16},{16,18},{18... | collective-permute-start | bytes 294920 | tf_op jit(solution)/shard_map/ppermute | solution.py:106
  355.5 6.8 %copy-start.28 = (bf16[96,512]{1,0:T(8,128)(2,1)S(1)}, bf16[96,512]{1,0:T(8,128)(2,1)}, u32[]{:S(2)}) copy-start(bf16[96,512]{1,0:T(8,128)(2,1)} %copy-done.27) | copy-start | bytes 294916
  355.5 6.8 %copy-start.26 = (bf16[96,512]{1,0:T(8,128)(2,1)S(1)}, bf16[96,512]{1,0:T(8,128)(2,1)}, u32[]{:S(2)}) copy-start(bf16[96,512]{1,0:T(8,128)(2,1)} %copy-done.25) | copy-start | bytes 294916
  355.5 7.0 %copy-start.12 = (bf16[96,512]{1,0:T(8,128)(2,1)S(1)}, bf16[96,512]{1,0:T(8,128)(2,1)}, u32[]{:S(2)}) copy-start(bf16[96,512]{1,0:T(8,128)(2,1)} %copy-done.11) | copy-start | bytes 294916
  355.5 7.0 %copy-start.10 = (bf16[96,512]{1,0:T(8,128)(2,1)S(1)}, bf16[96,512]{1,0:T(8,128)(2,1)}, u32[]{:S(2)}) copy-start(bf16[96,512]{1,0:T(8,128)(2,1)} %copy-done.9) | copy-start | bytes 294916
  355.5 7.0 %copy-start.8 = (bf16[96,512]{1,0:T(8,128)(2,1)S(1)}, bf16[96,512]{1,0:T(8,128)(2,1)}, u32[]{:S(2)}) copy-start(bf16[96,512]{1,0:T(8,128)(2,1)} %copy-done.7) | copy-start | bytes 294916
  355.5 7.0 %copy-start.5 = (f32[96,3072]{1,0:T(8,128)S(1)}, f32[96,3072]{1,0:T(8,128)}, u32[]{:S(2)}) copy-start(f32[96,3072]{1,0:T(8,128)} %reduce-scatter.2.cloned.1.call-done) | copy-start | bytes 3538948
  453.3 18.6 %copy-start.31 = (f32[512]{0:T(512)}, f32[512]{0:T(512)S(1)}, u32[]{:S(2)}) copy-start(f32[512]{0:T(512)S(1)} %maximum_multiply_fusion.2) | copy-start | bytes 6148
  457.6 14.3 %copy-start.32 = (f32[512]{0:T(512)}, f32[512]{0:T(512)S(1)}, u32[]{:S(2)}) copy-start(f32[512]{0:T(512)S(1)} %maximum_multiply_fusion.1) | copy-start | bytes 6148
  462.0 9.9 %copy-start.29 = (f32[2048]{0:T(1024)}, f32[2048]{0:T(1024)S(1)}, u32[]{:S(2)}) copy-start(f32[2048]{0:T(1024)S(1)} %maximum_multiply_fusion) | copy-start | bytes 24580
  (8 other events, 29.2 us)
Sparse Core Ops, SparseCore 0:
  64.9 194.4 reduce-scatter.1
  342.8 40.7 all-gather.3
